TPU v7x, 32 devices: a whole 2x2x4 slice. The times are simulated.
32 devices in a mesh: grp: 4 (over y, x), row: 8 (over z, core).
Axes of the slice: x: 2, y: 2, z: 4, core: 2. Of those that a mesh axis runs over, the one named last changes fastest.
Arguments:
- serving: bfloat16 [16384, 128], P('row'), may hold values from -1 to 1
- serving_scale: bfloat16 [128], P('row'), may hold values from 0.099609375 to 1
- hot_blocks: int32 [4, 16], P('grp', 'row'), may hold values from 0 to 15, as said below
- bag_lengths: int32 [32, 256], P(('grp', 'row')), may hold values from 1 to 16, 1024 in all within a row
- bag_indices: int32 [32, 1024], P(('grp', 'row')), may hold values from 0 to 2047, as said below
- dense_act: bfloat16 [8192, 128], P(('grp', 'row')), may hold values from -6 to 6
- labels: float32 [8192], P(('grp', 'row')), may hold values from 0 to 1
- w_top: bfloat16 [256, 1024], replicated, may hold values from -0.375 to 0.375
- w_out: float32 [1024], replicated, may hold values from -0.012 to 0.012
- master: float32 [4, 4096, 128], P('grp', 'row'), may hold values from -0.3 to 0.3
- accum: float32 [4, 4096], P('grp', 'row'), may hold values from 1e-05 to 0.0001
Outputs:
- new_master: float32 [4, 4096, 128], P('grp', 'row')
- new_accum: float32 [4, 4096], P('grp', 'row')
- new_serving: bfloat16 [16384, 128], P('row')
- new_scale: bfloat16 [128], P('row')
- top_grad: float32 [256, 1024], replicated
Inputs may be any that keep to these rules, and one draw needn't show every extreme that they name: `hot_blocks`: the 2 entries that one group names in one row shard are distinct. `bag_indices`: in each device's line, exactly 64 distinct values lie in each range of 256 consecutive positions that starts at a multiple of 256.
All inputs are finite; a program needn't handle non-finite values. Where the computation divides by a largest or mean magnitude, that divisor is 1e-20 or more.
Results may differ from a plain program's by a relative error of at most 0.012.
Values may be sent and summed in bfloat16 or wider, within the bound.
A program may use at most 128 MiB of HBM per device.

v0:
```python
import math
import jax
import jax.numpy as jnp
from jax import lax
from jax.sharding import PartitionSpec as P

BLOCK = 128
MOST = 16
lr_step = 0.05


def pool_grad(table, lengths, indices, dense_d, labels_d, w_top, w_out):
    rows, width = table.shape
    total = indices.shape[0]
    ends = jnp.cumsum(lengths)
    starts = ends - lengths
    slots = jnp.arange(MOST, dtype=jnp.int32)
    positions = jnp.minimum(starts[:, None] + slots[None, :], total - 1)
    picked = jnp.where(slots[None, :] < lengths[:, None], indices[positions], -1)
    span = math.gcd(rows, 2048)
    pieces = rows // span

    def count_block(first):
        columns = first + jnp.arange(span, dtype=jnp.int32)
        return jnp.sum((picked[:, :, None] == columns[None, None, :]).astype(jnp.bfloat16), axis=1)

    counts = lax.map(count_block, jnp.arange(pieces, dtype=jnp.int32) * span)
    table_blocks = table.reshape(pieces, span, width)

    def add_block(running, pair):
        block_counts, block_rows = pair
        return (
            running
            + jnp.dot(
                block_counts.astype(jnp.float32), block_rows, precision=lax.Precision.HIGHEST
            ),
            None,
        )

    pooled, _ = lax.scan(
        add_block, jnp.zeros((lengths.shape[0], width), jnp.float32), (counts, table_blocks)
    )
    joined = jnp.concatenate([pooled.astype(jnp.bfloat16), dense_d], axis=1)
    pre = jnp.dot(joined, w_top, preferred_element_type=jnp.float32)
    sig = jax.nn.sigmoid(pre)
    logit = jnp.dot(pre * sig, w_out, precision=lax.Precision.HIGHEST)
    dlogit = jax.nn.sigmoid(logit) - labels_d
    dpre = (dlogit[:, None] * w_out[None, :] * (sig * (1.0 + pre * (1.0 - sig)))).astype(
        jnp.bfloat16
    )
    top = lax.dot_general(
        joined, dpre, (((0,), (0,)), ((), ())), preferred_element_type=jnp.float32
    )
    dz = lax.dot_general(dpre, w_top, (((1,), (1,)), ((), ())), preferred_element_type=jnp.float32)
    emb_grad = dz[:, :width]

    def spread_block(block_counts):
        weights = block_counts.astype(jnp.float32)
        summed = lax.dot_general(
            weights, emb_grad, (((0,), (0,)), ((), ())), precision=lax.Precision.HIGHEST
        )
        return (summed, jnp.sum(weights, axis=0))

    hot, column_use = lax.map(spread_block, counts)
    return (top, hot.reshape(rows, width), column_use.reshape(rows) > 0)


def on_device(
    serving,
    serving_scale,
    hot_blocks,
    bag_lengths,
    bag_indices,
    dense_act,
    labels,
    w_top,
    w_out,
    master,
    accum,
):
    width = serving.shape[1]
    chosen = hot_blocks[0]
    count = chosen.shape[0]
    local_blocks = serving.reshape(-1, BLOCK, width)
    total_blocks = local_blocks.shape[0]
    picked = local_blocks[chosen]
    picked_scale = serving_scale[chosen]
    fetched, fetched_scale = (
        lax.all_gather(picked, "row", axis=0, tiled=True),
        lax.all_gather(picked_scale, "row", axis=0, tiled=True),
    )
    table = (
        fetched.astype(jnp.float32) * fetched_scale.astype(jnp.float32)[:, None, None]
    ).reshape(-1, width)
    top_part, hot_part, used_rows = pool_grad(
        table, bag_lengths[0], bag_indices[0], dense_act, labels, w_top, w_out
    )
    top_grad = lax.psum(top_part, ("grp", "row"))
    owned = lax.psum_scatter(hot_part, "row", scatter_dimension=0, tiled=True).reshape(
        count, BLOCK, width
    )
    quarter = lax.axis_index("grp")
    groups = lax.axis_size("grp")
    per_owner = total_blocks // groups
    arrived, arrived_ids = (
        lax.all_gather(owned, "grp", axis=0, tiled=True),
        lax.all_gather(chosen.astype(jnp.float32), "grp", axis=0, tiled=True),
    )
    slot = arrived_ids.astype(jnp.int32) - quarter * per_owner
    inside = (slot >= 0) & (slot < per_owner)
    slot = jnp.where(inside, slot, per_owner)
    grad = (
        jnp.zeros((per_owner, BLOCK, width), jnp.float32)
        .at[slot]
        .add(arrived, mode="drop")
        .reshape(-1, width)
    )
    weights = master[0]
    state = accum[0]
    new_state = state + jnp.mean(grad * grad, axis=1)
    new_weights = weights - lr_step * grad / jnp.sqrt(new_state)[:, None]
    scale_new = (
        jnp.max(jnp.abs(new_weights.reshape(per_owner, BLOCK * width)), axis=1) + 1e-06
    ).astype(jnp.bfloat16)
    coded = (
        (
            new_weights.reshape(per_owner, BLOCK, width)
            / scale_new.astype(jnp.float32)[:, None, None]
        )
        .astype(jnp.bfloat16)
        .reshape(-1, width)
    )
    fresh, fresh_scale = (
        lax.all_gather(coded, "grp", axis=0, tiled=True),
        lax.all_gather(scale_new, "grp", axis=0, tiled=True),
    )
    return (new_weights[None], new_state[None], fresh, fresh_scale, top_grad)


def solution(mesh):
    return jax.shard_map(
        on_device,
        mesh=mesh,
        in_specs=(
            P("row", None),
            P("row"),
            P("grp", "row"),
            P(("grp", "row"), None),
            P(("grp", "row"), None),
            P(("grp", "row"), None),
            P(("grp", "row")),
            P(),
            P(),
            P("grp", "row", None),
            P("grp", "row"),
        ),
        out_specs=(P("grp", "row", None), P("grp", "row"), P("row", None), P("row"), P()),
        check_vma=False,
    )
```

profile of v0, /device:TPU:0, one launch (start us, length us, event | category | flops | bytes accessed | tf_op | source)
XLA Modules:
  0.0 261.1 jit_solution(4268729098067179809)
XLA Ops:
  8.1 1.0 reduce-window.9
  9.3 0.8 bitcast_subtract_fusion
  10.4 16.7 %gather_fusion = s32[4096]{0:T(1024)S(1)} fusion(s32[1024]{0:T(1024)S(1)} %bitcast.46, s32[4096]{0:T(1024)S(1)} %broadcast_clamp_fusion), kind=kCustom, calls=%fused_computation | custom fusion | bytes 49152 | tf_op jit(solution)/shard_map/gather | solution.py:19
  27.3 0.6 dynamic-slice.2
  28.6 0.6 gather_fusion.2
  29.5 10.4 %fusion.1 = bf16[256,2048]{1,0:T(8,128)(2,1)S(1)} fusion(s32[256,16]{1,0:T(8,128)S(1)} %fusion.8), kind=kLoop, calls=%fused_computation.6 | loop fusion | flops 24641536 | bytes 1064960 | tf_op jit(solution)/shard_map/while/body/eval_jaxpr/reduce_sum | solution.py:25
  39.9 18.1 %all-reduce.1 = bf16[16]{0:T(256)(128)(2,1)S(1)} all-reduce(bf16[16]{0:T(256)(128)(2,1)S(1)} %dynamic-update-slice.1), channel_id=4, replica_groups=mesh['grp'=4,'row'=8] {'row'}, use_global_device_ids=true, to_apply=%add.1 | all-reduce | flops 16 | bytes 64
  58.0 0.6 gather_fusion.1
  58.6 15.1 %all-gather.1 = bf16[16,128,128]{2,1,0:T(8,128)(2,1)S(1)} all-gather(bf16[2,128,128]{2,1,0:T(8,128)(2,1)S(1)} %gather_fusion.1), channel_id=3, replica_groups=mesh['grp'=4,'row'=8] {'row'}, dimensions={0}, use_global_device_ids=true | all-gather | bytes 589824 | tf_op jit(solution)/shard_map/all_gather | solution.py:89
  74.0 1.0 convolution_convert_fusion
  75.0 0.3 fusion.10
  75.3 0.4 copy-done.9
  75.7 1.1 fusion.2
  76.8 0.4 multiply_convert_fusion
  77.2 0.3 fusion.5
  77.5 2.2 fusion.18
  79.8 0.6 copy-done.12
  80.3 0.6 dynamic-slice.1
  81.7 9.9 %all-reduce = f32[8]{0:T(128)S(1)} all-reduce(f32[8]{0:T(128)S(1)} %bitcast_dynamic-update-slice_fusion), channel_id=2, replica_groups=mesh['grp'=4,'row'=8] {'grp'}, use_global_device_ids=true, to_apply=%add | all-reduce | flops 8 | bytes 64
  92.2 1.3 fusion.9
  93.5 17.2 %reduce-scatter.2.cloned.1.call-done = f32[256,128]{1,0:T(8,128)} async-done(((f32[2048,128]{1,0:T(8,128)}), f32[256,128]{1,0:T(8,128)}) %reduce-scatter.2.cloned.1.call-update) | async-done | bytes 131088 | tf_op jit(solution)/shard_map/reduce_scatter | solution.py:99
  110.8 10.3 %all_gather.21 = f32[8,128,128]{2,1,0:T(8,128)S(1)} all-gather(f32[2,128,128]{2,1,0:T(8,128)} %bitcast.51), channel_id=1, replica_groups=mesh['grp'=4,'row'=8] {'grp'}, dimensions={0}, use_global_device_ids=true | all-gather | bytes 655360 | tf_op jit(solution)/shard_map/all_gather | solution.py:106
  121.1 1.0 scatter_fusion
  122.4 0.8 abs_reduce_fusion
  123.3 0.2 dynamic-update-slice.2
  123.6 9.6 %all-reduce.2 = bf16[16]{0:T(256)(128)(2,1)} all-reduce(bf16[16]{0:T(256)(128)(2,1)S(1)} %dynamic-update-slice.2), channel_id=1, replica_groups=mesh['grp'=4,'row'=8] {'grp'}, use_global_device_ids=true, to_apply=%add.2 | all-reduce | flops 16 | bytes 64
  133.4 9.7 %all_gather.22 = bf16[2048,128]{1,0:T(8,128)(2,1)S(1)} all-gather(bf16[512,128]{1,0:T(8,128)(2,1)S(1)} %bitcast.50), channel_id=1, replica_groups=mesh['grp'=4,'row'=8] {'grp'}, dimensions={0}, use_global_device_ids=true | all-gather | bytes 655360 | tf_op jit(solution)/shard_map/all_gather | solution.py:134
  143.1 0.6 add.103
  143.6 107.6 %all-reduce.5.cloned.1.call-done = f32[256,1024]{1,0:T(8,128)} async-done(((f32[256,1024]{1,0:T(8,128)}), f32[256,1024]{1,0:T(8,128)}) %all-reduce.5.cloned.1.call-update) | async-done | bytes 1048592 | tf_op jit(solution)/shard_map/psum | solution.py:98
  251.3 0.8 copy.26
  252.1 0.6 copy-done.5
  252.7 1.0 copy.27
  (56 shorter events, 1.9 us)
Async XLA Ops:
  8.0 50.0 %copy-start = (bf16[2048,128]{1,0:T(8,128)(2,1)S(1)}, bf16[2048,128]{1,0:T(8,128)(2,1)}, u32[]{:S(2)}) copy-start(bf16[2048,128]{1,0:T(8,128)(2,1)} %param.11) | copy-start | bytes 1572868
  8.0 2.3 copy-start.1
  8.0 102.7 %reduce-scatter.2.cloned.1.call-start = ((), (), s32[]{:S(2)}) async-start(), calls=%async_computation.1 | async-start | bytes 1179648 | tf_op jit(solution)/shard_map/reduce_scatter | solution.py:99
  10.3 16.8 %copy-start.8 = (s32[1,256]{1,0:T(1,128)S(1)}, s32[1,256]{1,0:T(1,128)}, u32[]{:S(2)}) copy-start(s32[1,256]{1,0:T(1,128)} %param.14) | copy-start | bytes 3076
  10.3 16.9 %copy-start.11 = (s32[1,2]{1,0:T(1,128)S(1)}, s32[1,2]{1,0:T(1,128)}, u32[]{:S(2)}) copy-start(s32[1,2]{1,0:T(1,128)} %param.13) | copy-start | bytes 28
  10.3 17.0 %copy-start.13 = (u32[32]{0:T(128)S(1)}, u32[32]{0:T(128)}, u32[]{:S(2)}) copy-start(u32[32]{0:T(128)} %constant.82) | copy-start | bytes 388
  10.4 18.2 %copy-start.2 = (bf16[16]{0:T(256)(128)(2,1)S(1)}, bf16[16]{0:T(256)(128)(2,1)}, u32[]{:S(2)}) copy-start(bf16[16]{0:T(256)(128)(2,1)} %param.12) | copy-start | bytes 100
  29.2 44.5 %copy-start.6 = (bf16[256,128]{1,0:T(8,128)(2,1)S(1)}, bf16[256,128]{1,0:T(8,128)(2,1)}, u32[]{:S(2)}) copy-start(bf16[256,128]{1,0:T(8,128)(2,1)} %param.16) | copy-start | bytes 196612
  73.9 1.0 copy-start.3
  75.0 0.7 copy-start.9
  75.7 1.1 copy-start.10
  79.7 0.7 copy-start.12
  79.7 171.5 %all-reduce.5.cloned.1.call-start = ((), (), s32[]{:S(2)}) async-start(), calls=%async_computation.2 | async-start | bytes 2097152 | tf_op jit(solution)/shard_map/psum | solution.py:98
  121.1 1.2 copy-start.7
  121.1 1.2 copy-start.4
  251.3 1.4 copy-start.5
Sparse Core Ops, SparseCore 0:
  79.8 30.8 reduce-scatter.1
Sparse Core Ops, SparseCore 1:
  123.7 127.5 all-reduce.4
where the time goes:
time: 262 us; the launch traced here: 261 us
  waiting for transfers between devices  125 us (48%)
  blocking collectives  72.7 us (28%)
  local copies, waits for them, and re-layouts  23.5 us (9%)
  between operations  17.8 us (7%)
  other arithmetic  16 us (6%)
  matrix products  6.17 us (2%)
    psum x1, waiting for transfers between devices, on_device(): top_grad = lax.psum(top_part, ('grp', 'row'))  108 us
    unnamed x3, blocking collectives  37.6 us
    reduce_scatter x1, waiting for transfers between devices, on_device(): lax.psum_scatter(hot_part, 'row', scatter_dimension=0, tiled=True)  17.2 us
    gather x2, local copies, waits for them, and re-layouts, pool_grad(): indices[positions]  16.8 us
    all_gather x1, blocking collectives, on_device(): lax.all_gather(picked, 'row', axis=0, tiled=True)  15.1 us
    reduce_sum x1, other arithmetic, count_block(): jnp.sum((picked[:, :, None] == columns[None, None, :]).astype(jnp.bfloat1...  10.4 us
    all_gather x1, blocking collectives, on_device(): lax.all_gather(owned, 'grp', axis=0, tiled=True)  10.3 us
    all_gather x1, blocking collectives, on_device(): lax.all_gather(coded, 'grp', axis=0, tiled=True)  9.65 us
  transfers between devices with their start and end apart: 2, of which 2 were waited for; matrix products, arithmetic and copies ran while one was open for 1% of the time, Pallas kernels for 0%

commit v1 on v0

--- a/solution.py
+++ b/solution.py
@@ -95,7 +95,7 @@
     top_part, hot_part, used_rows = pool_grad(
         table, bag_lengths[0], bag_indices[0], dense_act, labels, w_top, w_out
     )
-    top_grad = lax.psum(top_part, ("grp", "row"))
+    top_grad = jnp.sum(lax.all_gather(top_part, ("grp", "row")), axis=0)
     owned = lax.psum_scatter(hot_part, "row", scatter_dimension=0, tiled=True).reshape(
         count, BLOCK, width
     )

time: 262 us -> 311 us (1.19)
  waiting for transfers between devices: 125 us -> 152 us
  other arithmetic: 16 us -> 29.5 us
  blocking collectives: 72.7 us -> 81.3 us
    all_gather x0 -> x1, waiting for transfers between devices: none -> 121 us  [on_device(): top_grad = jnp.sum(lax.all_gather(top_part, ('grp', 'row')), axis=0)]
    psum x1 -> x0, waiting for transfers between devices: 108 us -> none  [on_device(): top_grad = lax.psum(top_part, ('grp', 'row'))]
    reduce_scatter x1, waiting for transfers between devices: 17.2 us -> 31.6 us  [on_device(): lax.psum_scatter(hot_part, 'row', scatter_dimension=0, tiled=True)]
    reduce_sum x0 -> x1, other arithmetic: none -> 12.8 us  [on_device(): top_grad = jnp.sum(lax.all_gather(top_part, ('grp', 'row')), axis=0)]
    all_gather x1, blocking collectives: 10.3 us -> 16.5 us  [on_device(): lax.all_gather(owned, 'grp', axis=0, tiled=True)]
  transfers between devices with their start and end apart: 2 -> 2, of which waited for: 2 -> 2; matrix products, arithmetic and copies ran while one was open for 1% -> 2% of each run, Pallas kernels for 0% -> 0%
where the time goes in v1:
time: 311 us; the launch traced here: 310 us
  waiting for transfers between devices  152 us (49%)
  blocking collectives  81.3 us (26%)
  other arithmetic  29.5 us (9%)
  local copies, waits for them, and re-layouts  23 us (7%)
  between operations  17.7 us (6%)
  matrix products  6.34 us (2%)
    all_gather x1, waiting for transfers between devices, on_device(): top_grad = jnp.sum(lax.all_gather(top_part, ('grp', 'row')), axis=0)  121 us
    unnamed x3, blocking collectives  37.9 us
    reduce_scatter x1, waiting for transfers between devices, on_device(): lax.psum_scatter(hot_part, 'row', scatter_dimension=0, tiled=True)  31.6 us
    gather x2, local copies, waits for them, and re-layouts, pool_grad(): indices[positions]  16.8 us
    all_gather x1, blocking collectives, on_device(): lax.all_gather(owned, 'grp', axis=0, tiled=True)  16.5 us
    all_gather x1, blocking collectives, on_device(): lax.all_gather(picked, 'row', axis=0, tiled=True)  14.9 us
    reduce_sum x1, other arithmetic, on_device(): top_grad = jnp.sum(lax.all_gather(top_part, ('grp', 'row')), axis=0)  12.8 us
    all_gather x1, blocking collectives, on_device(): lax.all_gather(coded, 'grp', axis=0, tiled=True)  12 us
  transfers between devices with their start and end apart: 2, of which 2 were waited for; matrix products, arithmetic and copies ran while one was open for 2% of the time, Pallas kernels for 0%

profile of v1, /device:TPU:0, one launch (start us, length us, event | category | flops | bytes accessed | tf_op | source)
XLA Modules:
  0.0 310.1 jit_solution(13665816136296797830)
XLA Ops:
  8.1 0.7 fusion.12
  8.8 1.0 reduce-window.9
  9.9 1.2 dynamic-slice.2
  11.8 1.3 gather_fusion.2
  13.1 0.2 dynamic-update-slice.1
  13.4 18.1 %all-reduce.1 = bf16[16]{0:T(256)(128)(2,1)S(1)} all-reduce(bf16[16]{0:T(256)(128)(2,1)S(1)} %dynamic-update-slice.1), channel_id=4, replica_groups=mesh['grp'=4,'row'=8] {'row'}, use_global_device_ids=true, to_apply=%add.1 | all-reduce | flops 16 | bytes 64
  31.5 0.6 gather_fusion.1
  32.1 0.9 copy.19
  33.0 0.8 bitcast_subtract_fusion
  34.1 16.7 %gather_fusion = s32[4096]{0:T(1024)S(1)} fusion(s32[1024]{0:T(1024)S(1)} %bitcast.47, s32[4096]{0:T(1024)S(1)} %broadcast_clamp_fusion), kind=kCustom, calls=%fused_computation | custom fusion | bytes 49152 | tf_op jit(solution)/shard_map/gather | solution.py:19
  51.0 14.9 %all-gather.1 = bf16[16,128,128]{2,1,0:T(8,128)(2,1)S(1)} all-gather(bf16[2,128,128]{2,1,0:T(8,128)(2,1)S(1)} %gather_fusion.1), channel_id=3, replica_groups=mesh['grp'=4,'row'=8] {'row'}, dimensions={0}, use_global_device_ids=true | all-gather | bytes 589824 | tf_op jit(solution)/shard_map/all_gather | solution.py:89
  66.0 10.4 %fusion.1 = bf16[256,2048]{1,0:T(8,128)(2,1)S(1)} fusion(s32[256,16]{1,0:T(8,128)S(1)} %fusion.8), kind=kLoop, calls=%fused_computation.6 | loop fusion | flops 24641536 | bytes 1064960 | tf_op jit(solution)/shard_map/while/body/eval_jaxpr/reduce_sum | solution.py:25
  76.5 1.0 convolution_convert_fusion
  77.5 0.5 fusion.10
  78.0 1.1 fusion.2
  79.1 0.4 multiply_convert_fusion
  79.6 0.3 fusion.5
  79.9 2.2 fusion.18
  82.1 1.3 fusion.9
  83.4 0.6 dynamic-slice.1
  84.8 9.9 %all-reduce = f32[8]{0:T(128)S(1)} all-reduce(f32[8]{0:T(128)S(1)} %bitcast_dynamic-update-slice_fusion), channel_id=2, replica_groups=mesh['grp'=4,'row'=8] {'grp'}, use_global_device_ids=true, to_apply=%add | all-reduce | flops 8 | bytes 64
  95.4 31.6 %reduce-scatter.2.cloned.1.call-done = f32[256,128]{1,0:T(8,128)} async-done(((f32[2048,128]{1,0:T(8,128)}), f32[256,128]{1,0:T(8,128)}) %reduce-scatter.2.cloned.1.call-update) | async-done | bytes 131088 | tf_op jit(solution)/shard_map/reduce_scatter | solution.py:99
  126.9 16.5 %all_gather.27 = f32[8,128,128]{2,1,0:T(8,128)S(1)} all-gather(f32[2,128,128]{2,1,0:T(8,128)} %bitcast.53), channel_id=1, replica_groups=mesh['grp'=4,'row'=8] {'grp'}, dimensions={0}, use_global_device_ids=true | all-gather | bytes 655360 | tf_op jit(solution)/shard_map/all_gather | solution.py:106
  143.4 1.0 scatter_fusion
  144.7 0.8 abs_reduce_fusion
  145.6 0.2 dynamic-update-slice.2
  145.9 9.9 %all-reduce.2 = bf16[16]{0:T(256)(128)(2,1)} all-reduce(bf16[16]{0:T(256)(128)(2,1)S(1)} %dynamic-update-slice.2), channel_id=1, replica_groups=mesh['grp'=4,'row'=8] {'grp'}, use_global_device_ids=true, to_apply=%add.2 | all-reduce | flops 16 | bytes 64
  155.8 0.6 add.101
  156.5 12.0 %all_gather.28 = bf16[2048,128]{1,0:T(8,128)(2,1)S(1)} all-gather(bf16[512,128]{1,0:T(8,128)(2,1)S(1)} %bitcast.52), channel_id=1, replica_groups=mesh['grp'=4,'row'=8] {'grp'}, dimensions={0}, use_global_device_ids=true | all-gather | bytes 655360 | tf_op jit(solution)/shard_map/all_gather | solution.py:134
  168.5 120.6 %all-gather.6.cloned.1.call-done = f32[8192,1024]{1,0:T(8,128)} async-done(((f32[256,1024]{1,0:T(8,128)}), f32[8192,1024]{1,0:T(8,128)}) %all-gather.6.cloned.1.call-update) | async-done | bytes 33554448 | tf_op jit(solution)/shard_map/all_gather | solution.py:98
  289.1 12.8 %reduce_sum.33 = f32[256,1024]{1,0:T(8,128)} reduce(f32[32,256,1024]{2,1,0:T(8,128)} %bitcast.48, f32[]{:T(128)} %constant.20.clone.1), dimensions={0}, to_apply=%region_8.9 | reduce | flops 8126464 | bytes 34603012 | tf_op jit(solution)/shard_map/reduce_sum | solution.py:98
  301.9 0.8 copy.25
  (48 shorter events, 1.5 us)
Async XLA Ops:
  8.0 23.5 %copy-start = (bf16[2048,128]{1,0:T(8,128)(2,1)S(1)}, bf16[2048,128]{1,0:T(8,128)(2,1)}, u32[]{:S(2)}) copy-start(bf16[2048,128]{1,0:T(8,128)(2,1)} %param.11) | copy-start | bytes 1572868
  8.0 26.0 %copy-start.1 = (s32[1,1024]{1,0:T(1,128)S(1)}, s32[1,1024]{1,0:T(1,128)}, u32[]{:S(2)}) copy-start(s32[1,1024]{1,0:T(1,128)} %param.15) | copy-start | bytes 12292
  8.0 118.9 %reduce-scatter.2.cloned.1.call-start = ((), (), s32[]{:S(2)}) async-start(), calls=%async_computation.1 | async-start | bytes 1179648 | tf_op jit(solution)/shard_map/reduce_scatter | solution.py:99
  34.0 16.9 %copy-start.5 = (s32[1,256]{1,0:T(1,128)S(1)}, s32[1,256]{1,0:T(1,128)}, u32[]{:S(2)}) copy-start(s32[1,256]{1,0:T(1,128)} %param.14) | copy-start | bytes 3076
  34.0 43.5 %copy-start.2 = (bf16[256,1024]{1,0:T(8,128)(2,1)S(1)}, bf16[256,1024]{1,0:T(8,128)(2,1)}, u32[]{:S(2)}) copy-start(bf16[256,1024]{1,0:T(8,128)(2,1)} %param.18) | copy-start | bytes 1572868
  34.1 44.0 %copy-start.6 = (f32[1024]{0:T(1024)S(1)}, f32[1024]{0:T(1024)}, u32[]{:S(2)}) copy-start(f32[1024]{0:T(1024)} %param.19) | copy-start | bytes 12292
  34.1 45.1 %copy-start.7 = (f32[256]{0:T(256)S(1)}, f32[256]{0:T(256)}, u32[]{:S(2)}) copy-start(f32[256]{0:T(256)} %param.17) | copy-start | bytes 3076
  34.1 49.4 %copy-start.9 = (u32[32]{0:T(128)S(1)}, u32[32]{0:T(128)}, u32[]{:S(2)}) copy-start(u32[32]{0:T(128)} %constant.77) | copy-start | bytes 388
  34.1 50.6 %copy-start.8 = (s32[1,2]{1,0:T(1,128)S(1)}, s32[1,2]{1,0:T(1,128)}, u32[]{:S(2)}) copy-start(s32[1,2]{1,0:T(1,128)} %param.13) | copy-start | bytes 28
  34.1 110.5 %copy-start.4 = (f32[1,512]{1,0:T(1,128)S(1)}, f32[1,512]{1,0:T(1,128)}, u32[]{:S(2)}) copy-start(f32[1,512]{1,0:T(1,128)} %param.21) | copy-start | bytes 6148
  34.1 110.5 %copy-start.3 = (f32[1,512,128]{2,1,0:T(8,128)S(1)}, f32[1,512,128]{2,1,0:T(8,128)}, u32[]{:S(2)}) copy-start(f32[1,512,128]{2,1,0:T(8,128)} %param.20) | copy-start | bytes 786436
  82.1 207.0 %all-gather.6.cloned.1.call-start = ((), (), s32[]{:S(2)}) async-start(), calls=%async_computation.2 | async-start | bytes 34603008 | tf_op jit(solution)/shard_map/all_gather | solution.py:98
Sparse Core Ops, SparseCore 0:
  82.2 44.7 reduce-scatter.1
Sparse Core Ops, SparseCore 1:
  85.6 203.5 all-gather.5
